TPU v7x, 32 devices: a whole 2x2x4 slice. The times are simulated.
32 devices in a mesh: dp: 4 (over y, x), centers: 8 (over z, core).
Axes of the slice: x: 2, y: 2, z: 4, core: 2. Of those that a mesh axis runs over, the one named last changes fastest.
Arguments:
- points: bfloat16 [16384, 32], P('dp'), may hold values from -6 to 6
- centers: bfloat16 [16384, 32], P('centers'), may hold values from -6 to 6
- coef: bfloat16 [16384, 64], P('centers'), may hold values from -0.1875 to 0.1875
Outputs:
- product: float32 [16384, 64], P('centers')
All inputs are finite; a program needn't handle non-finite values.
Results may differ from a plain program's by a relative error of at most 0.0003.
Values may be sent and summed in bfloat16 or wider, within the bound.
No kernel may reach another device: no remote copies, remote signals or barrier semaphores. Data moves between devices by JAX's collectives and lax.ppermute only.
A program may use at most 128 MiB of HBM per device.

v0:
```python
import jax
import jax.numpy as jnp
from jax import lax
from jax.sharding import PartitionSpec as P


def kernel_block(left_pts, left_sq, right_pts, right_sq, features):
    inner = lax.dot_general(
        left_pts, right_pts, (((1,), (1,)), ((), ())), preferred_element_type=jnp.float32
    )
    dist = left_sq[:, None] + right_sq[None, :] - 2.0 * inner
    return jnp.exp(dist * (-2.0 / features)).astype(jnp.bfloat16)


def squares(values):
    wide = values.astype(jnp.float32)
    return jnp.sum(wide * wide, axis=1)


def on_device(points, centers, coef):
    features = points.shape[1]
    local_pts = points.shape[0]
    local_cen = centers.shape[0]
    outs_count = coef.shape[1]
    block_pts = min(1024, local_pts)
    block_count = local_pts // block_pts
    cen_sq = squares(centers)
    point_blocks = points.reshape(block_count, block_pts, features)
    scalar_zero = jnp.zeros((), jnp.float32)

    def forward_keep(carry, block):
        kernel = kernel_block(block, squares(block), centers, cen_sq, features)
        return (carry, (kernel, jnp.dot(kernel, coef, preferred_element_type=jnp.float32)))

    unused, (tiles, partial_value) = lax.scan(forward_keep, scalar_zero, point_blocks)
    forward_part = partial_value.reshape(local_pts, outs_count)
    shared = lax.psum_scatter(
        forward_part.astype(jnp.bfloat16), "centers", scatter_dimension=0, tiled=True
    )
    forward = lax.all_gather(shared, "centers", axis=0, tiled=True)
    forward_blocks = forward.reshape(block_count, block_pts, outs_count)
    back = jnp.einsum("bij,bio->jo", tiles, forward_blocks, preferred_element_type=jnp.float32)
    total_pts = local_pts * lax.axis_size("dp")
    back = back * (1.0 / jnp.sqrt(jnp.float32(total_pts)))
    own_count = local_cen // lax.axis_size("dp")
    own_start = lax.axis_index("dp") * own_count
    own_cen = lax.dynamic_slice_in_dim(centers, own_start, own_count, 0)
    own_sq = squares(own_cen)
    piece_cen = lax.all_gather(centers, "centers", axis=0, tiled=True)
    piece_coef = lax.all_gather(coef, "centers", axis=0, tiled=True)
    kernel = kernel_block(own_cen, own_sq, piece_cen, squares(piece_cen), features)
    regular = jnp.dot(kernel, piece_coef, preferred_element_type=jnp.float32)
    placed = lax.dynamic_update_slice_in_dim(jnp.zeros_like(back), regular, own_start, 0)
    return lax.psum(back + placed, "dp")


def solution(mesh):
    in_specs = (P("dp", None), P("centers", None), P("centers", None))
    out_specs = P("centers", None)
    return jax.shard_map(
        on_device, mesh=mesh, in_specs=in_specs, out_specs=out_specs, check_vma=False
    )
```

profile of v0, /device:TPU:0, one launch (start us, length us, event | category | flops | bytes accessed | tf_op | source)
XLA Modules:
  0.0 192.9 jit_solution(11572367523075643524)
XLA Ops:
  6.5 0.0 reduce-scatter.2.cloned.1.call-start
  6.5 1.4 copy.5
  8.0 1.0 multiply_reduce_fusion.2
  8.9 27.9 %while.12 = (s32[]{:T(128)}, bf16[4,1024,2048]{2,1,0:T(8,128)(2,1)}, bf16[4,1024,64]{1,2,0:T(8,128)(2,1)S(1)}, bf16[4,1024,32]{2,1,0:T(8,128)(2,1)S(1)}, f32[204...) while((s32[]{:T(128)}, bf16[4,1024,2048]{2,1,0:T(8,128)(2,1)}, ...), condition=%wide.region_3.4_spmd, body=%wide.region_1.3_spmd.sunk | while | flops 413236224 | bytes 13583461 | solution.py:35
  8.9 0.2 multiply_reduce_fusion.5
  9.2 4.4 %bitcast_dynamic-update-slice_fusion.2 = (bf16[4,1024,2048]{2,1,0:T(8,128)(2,1)}, bf16[1024,2048]{1,0:T(8,128)(2,1)S(1)}) fusion(bf16[4,1024,2048]{2,1,0:T(8,128)(2,1)} %get-tuple-element.117, s32[]{:T(128)S(6)} %copy.19, bf16[2048,32]{0,1:T(8,128)(2,1)} %get-tuple-element.129, bf16[4,1024,32]{2,1,0:T(8,128)(2,1)S(1)} %get-tuple-element.127, ...), kind=kOutput, calls=%fused_computation.1.clone.1 | convolution fusion | flops 144703488 | bytes 8795136 | tf_op jit(solution)/shard_map/while/body/eval_jaxpr/dot_general | solution.py:8
  13.5 2.3 %fusion.29 = bf16[4,1024,64]{1,2,0:T(8,128)(2,1)S(1)} fusion(bf16[4,1024,64]{1,2,0:T(8,128)(2,1)S(1)} %get-tuple-element.118, s32[]{:T(128)S(6)} %copy.19, bf16[1024,2048]{1,0:T(8,128)(2,1)S(1)} %get-tuple-element.107, bf16[2048,64]{0,1:T(8,128)(2,1)} %get-tuple-element.130), kind=kOutput, calls=%fused_computation.3.clone.1 | convolution fusion | flops 268435456 | bytes 4718596 | tf_op jit(solution)/shard_map/while/body/eval_jaxpr/dot_general | solution.py:33
  15.9 0.2 multiply_reduce_fusion.5
  16.1 4.4 %bitcast_dynamic-update-slice_fusion.2 = (bf16[4,1024,2048]{2,1,0:T(8,128)(2,1)}, bf16[1024,2048]{1,0:T(8,128)(2,1)S(1)}) fusion(bf16[4,1024,2048]{2,1,0:T(8,128)(2,1)} %get-tuple-element.117, s32[]{:T(128)S(6)} %copy.19, bf16[2048,32]{0,1:T(8,128)(2,1)} %get-tuple-element.129, bf16[4,1024,32]{2,1,0:T(8,128)(2,1)S(1)} %get-tuple-element.127, ...), kind=kOutput, calls=%fused_computation.1.clone.1 | convolution fusion | flops 144703488 | bytes 8795136 | tf_op jit(solution)/shard_map/while/body/eval_jaxpr/dot_general | solution.py:8
  20.5 2.3 %fusion.29 = bf16[4,1024,64]{1,2,0:T(8,128)(2,1)S(1)} fusion(bf16[4,1024,64]{1,2,0:T(8,128)(2,1)S(1)} %get-tuple-element.118, s32[]{:T(128)S(6)} %copy.19, bf16[1024,2048]{1,0:T(8,128)(2,1)S(1)} %get-tuple-element.107, bf16[2048,64]{0,1:T(8,128)(2,1)} %get-tuple-element.130), kind=kOutput, calls=%fused_computation.3.clone.1 | convolution fusion | flops 268435456 | bytes 4718596 | tf_op jit(solution)/shard_map/while/body/eval_jaxpr/dot_general | solution.py:33
  22.9 0.2 multiply_reduce_fusion.5
  23.1 4.4 %bitcast_dynamic-update-slice_fusion.2 = (bf16[4,1024,2048]{2,1,0:T(8,128)(2,1)}, bf16[1024,2048]{1,0:T(8,128)(2,1)S(1)}) fusion(bf16[4,1024,2048]{2,1,0:T(8,128)(2,1)} %get-tuple-element.117, s32[]{:T(128)S(6)} %copy.19, bf16[2048,32]{0,1:T(8,128)(2,1)} %get-tuple-element.129, bf16[4,1024,32]{2,1,0:T(8,128)(2,1)S(1)} %get-tuple-element.127, ...), kind=kOutput, calls=%fused_computation.1.clone.1 | convolution fusion | flops 144703488 | bytes 8795136 | tf_op jit(solution)/shard_map/while/body/eval_jaxpr/dot_general | solution.py:8
  27.5 2.3 %fusion.29 = bf16[4,1024,64]{1,2,0:T(8,128)(2,1)S(1)} fusion(bf16[4,1024,64]{1,2,0:T(8,128)(2,1)S(1)} %get-tuple-element.118, s32[]{:T(128)S(6)} %copy.19, bf16[1024,2048]{1,0:T(8,128)(2,1)S(1)} %get-tuple-element.107, bf16[2048,64]{0,1:T(8,128)(2,1)} %get-tuple-element.130), kind=kOutput, calls=%fused_computation.3.clone.1 | convolution fusion | flops 268435456 | bytes 4718596 | tf_op jit(solution)/shard_map/while/body/eval_jaxpr/dot_general | solution.py:33
  29.8 0.2 multiply_reduce_fusion.5
  30.1 4.4 %bitcast_dynamic-update-slice_fusion.2 = (bf16[4,1024,2048]{2,1,0:T(8,128)(2,1)}, bf16[1024,2048]{1,0:T(8,128)(2,1)S(1)}) fusion(bf16[4,1024,2048]{2,1,0:T(8,128)(2,1)} %get-tuple-element.117, s32[]{:T(128)S(6)} %copy.19, bf16[2048,32]{0,1:T(8,128)(2,1)} %get-tuple-element.129, bf16[4,1024,32]{2,1,0:T(8,128)(2,1)S(1)} %get-tuple-element.127, ...), kind=kOutput, calls=%fused_computation.1.clone.1 | convolution fusion | flops 144703488 | bytes 8795136 | tf_op jit(solution)/shard_map/while/body/eval_jaxpr/dot_general | solution.py:8
  34.5 2.3 %fusion.29 = bf16[4,1024,64]{1,2,0:T(8,128)(2,1)S(1)} fusion(bf16[4,1024,64]{1,2,0:T(8,128)(2,1)S(1)} %get-tuple-element.118, s32[]{:T(128)S(6)} %copy.19, bf16[1024,2048]{1,0:T(8,128)(2,1)S(1)} %get-tuple-element.107, bf16[2048,64]{0,1:T(8,128)(2,1)} %get-tuple-element.130), kind=kOutput, calls=%fused_computation.3.clone.1 | convolution fusion | flops 268435456 | bytes 4718596 | tf_op jit(solution)/shard_map/while/body/eval_jaxpr/dot_general | solution.py:33
  36.8 0.8 copy.9
  37.7 0.0 reduce-scatter.2.cloned.1.call-update
  37.7 0.0 all-gather.3.cloned.1.call-start
  37.7 0.7 all-gather.3.cloned.1.call-update
  38.4 0.0 all-gather.5.cloned.1.call-start
  38.5 0.7 all-gather.5.cloned.1.call-update
  39.2 0.0 all-reduce.2.cloned.1.call-start
  39.2 0.8 multiply_reduce_fusion.3
  40.0 31.9 %reduce-scatter.2.cloned.1.call-done = bf16[512,64]{0,1:T(8,128)(2,1)} async-done(((bf16[4096,64]{0,1:T(8,128)(2,1)}), bf16[512,64]{0,1:T(8,128)(2,1)}) %reduce-scatter.2.cloned.1.call-update) | async-done | bytes 65552 | tf_op jit(solution)/shard_map/reduce_scatter | solution.py:37
  71.9 16.8 %all_gather.9 = bf16[4096,64]{0,1:T(8,128)(2,1)S(1)} all-gather(bf16[512,64]{0,1:T(8,128)(2,1)} %reduce-scatter.2.cloned.1.call-done), channel_id=1, replica_groups=mesh['dp'=4,'centers'=8] {'centers'}, dimensions={0}, use_global_device_ids=true | all-gather | bytes 589824 | tf_op jit(solution)/shard_map/all_gather | solution.py:40
  88.7 8.9 %fusion.5 = f32[2048,64]{0,1:T(8,128)S(1)} fusion(bf16[4,1024,2048]{2,1,0:T(8,128)(2,1)} %get-tuple-element.43, bf16[8,4,8,1024]{3,2,1,0:T(8,128)(2,1)S(1)} %bitcast.46), kind=kOutput, calls=%fused_computation.11 | convolution fusion | flops 1073872896 | bytes 17825792 | tf_op jit(solution)/shard_map/bij,bio->jo/dot_general | solution.py:42
  97.6 0.0 all-gather.3.cloned.1.call-done
  97.6 1.5 multiply_reduce_fusion.1
  99.2 26.4 %all-gather.5.cloned.1.call-done = bf16[16384,64]{0,1:T(8,128)(2,1)} async-done(((bf16[2048,64]{0,1:T(8,128)(2,1)}), bf16[16384,64]{0,1:T(8,128)(2,1)}) %all-gather.5.cloned.1.call-update) | async-done | bytes 2097168 | tf_op jit(solution)/shard_map/all_gather | solution.py:50
  125.6 13.2 %fusion.7 = f32[2048,64]{0,1:T(8,128)S(1)} fusion(f32[2048,64]{0,1:T(8,128)S(1)} %fusion.5, s32[]{:T(128)S(6)} %select_n.4, bf16[16384,64]{0,1:T(8,128)(2,1)} %all-gather.5.cloned.1.call-done, bf16[16384,32]{0,1:T(8,128)(2,1)} %all-gather.3.cloned.1.call-done, f32[16384]{0:T(1024)S(1)} %multiply_reduce_fusion.1, f32[512]{0:T(512)S(1)} %multiply_reduce_fusion.3, ...), kind=kOutput, calls=%fused_computation.14 | convolution fusion | flops 1652588544 | bytes 3509248 | tf_op jit(solution)/shard_map/dot_general | solution.py:52
  138.8 0.0 copy-start
  138.8 0.8 copy-done
  139.6 0.0 all-reduce.2.cloned.1.call-update
  139.6 44.9 %all-reduce.2.cloned.1.call-done = f32[2048,64]{0,1:T(8,128)} async-done(((f32[2048,64]{0,1:T(8,128)}), f32[2048,64]{0,1:T(8,128)}) %all-reduce.2.cloned.1.call-update) | async-done | bytes 524304 | tf_op jit(solution)/shard_map/psum | solution.py:54
  184.5 1.9 copy.27
  (2 shorter events, 0.0 us)
Async XLA Ops:
  6.5 65.4 %reduce-scatter.2.cloned.1.call-start = ((), (), s32[]{:S(2)}) async-start(), calls=%async_computation.1 | async-start | bytes 589824 | tf_op jit(solution)/shard_map/reduce_scatter | solution.py:37
  37.7 59.9 %all-gather.3.cloned.1.call-start = ((), (), s32[]{:S(2)}) async-start(), calls=%async_computation.2 | async-start | bytes 1179648 | tf_op jit(solution)/shard_map/all_gather | solution.py:49
  38.4 87.2 %all-gather.5.cloned.1.call-start = ((), (), s32[]{:S(2)}) async-start(), calls=%async_computation.3 | async-start | bytes 2359296 | tf_op jit(solution)/shard_map/all_gather | solution.py:50
  39.2 145.4 %all-reduce.2.cloned.1.call-start = ((), (), s32[]{:S(2)}) async-start(), calls=%async_computation.4 | async-start | bytes 1048576 | tf_op jit(solution)/shard_map/psum | solution.py:54
  138.8 0.8 copy-start
Sparse Core Ops, SparseCore 0:
  37.8 34.0 reduce-scatter.1
  73.5 21.7 all-gather.2
  96.9 28.6 all-gather.4
  139.7 44.7 all-reduce.1
where the time goes:
time: 193 us
  waiting for transfers between devices  105 us (54%)
  matrix products  49 us (25%)
  blocking collectives  16.8 us (9%)
  between operations  13.2 us (7%)
  local copies, waits for them, and re-layouts  4.92 us (3%)
  other arithmetic  4.13 us (2%)
    psum x1, waiting for transfers between devices, on_device(): return lax.psum(back + placed, 'dp')  44.9 us
    reduce_scatter x1, waiting for transfers between devices, on_device(): lax.psum_scatter(forward_part.astype(jnp.bfloat16), 'centers', scatter_di...  31.9 us
    all_gather x1, waiting for transfers between devices, on_device(): piece_coef = lax.all_gather(coef, 'centers', axis=0, tiled=True)  26.4 us
    dot_general x4, matrix products, kernel_block(): lax.dot_general(left_pts, right_pts, (((1,), (1,)), ((), ())), preferred_...  17.6 us
    all_gather x1, blocking collectives, on_device(): forward = lax.all_gather(shared, 'centers', axis=0, tiled=True)  16.8 us
    dot_general x1, matrix products, on_device(): regular = jnp.dot(kernel, piece_coef, preferred_element_type=jnp.float32)  13.2 us
    dot_general x4, matrix products, forward_keep(): jnp.dot(kernel, coef, preferred_element_type=jnp.float32)  9.35 us
    dot_general x1, matrix products, on_device(): jnp.einsum('bij,bio->jo', tiles, forward_blocks, preferred_element_type=j...  8.89 us
  transfers between devices with their start and end apart: 4, of which 3 were waited for; matrix products, arithmetic and copies ran while one was open for 6% of the time, Pallas kernels for 0%

commit v1 on v0

v1 whole, which is shorter than its diff:
```python
import math

import jax
import jax.numpy as jnp
from jax import lax
from jax.experimental import pallas as pl
from jax.experimental.pallas import tpu as pltpu
from jax.sharding import PartitionSpec as P


TILE = 16
ROW_BLOCK = 512
COL_BLOCK = 512


def prepare(feats, values):
    count = len(feats)

    def body(*refs):
        for at in range(count):
            feat_ref, out_ref = refs[at], refs[count + len(present) + at]
            features, cols = feat_ref.shape
            wide = feat_ref[...].astype(jnp.float32)
            half = -0.5 * jnp.sum(wide * wide, axis=0, keepdims=True)
            high = half.astype(jnp.bfloat16).astype(jnp.float32)
            rest = half - high
            mid = rest.astype(jnp.bfloat16).astype(jnp.float32)
            low = rest - mid
            row = lax.broadcasted_iota(jnp.int32, (TILE, cols), 0)
            norm = jnp.where(row == 0, high, jnp.where(row == 1, mid, jnp.where(row == 2, low, 0.0)))
            out_ref[0:features, :] = feat_ref[...]
            out_ref[features : features + TILE, :] = norm.astype(jnp.bfloat16)
            if values[at] is not None:
                out_ref[features + TILE :, :] = refs[count + present.index(at)][...]

    present = [at for at in range(count) if values[at] is not None]
    shapes = [
        (feat.shape[0] + TILE + (0 if value is None else value.shape[0]), feat.shape[1])
        for feat, value in zip(feats, values)
    ]
    return pl.pallas_call(
        body,
        out_shape=[jax.ShapeDtypeStruct(shape, jnp.bfloat16) for shape in shapes],
    )(*feats, *[values[at] for at in present])


def product(rows, right, features, acc=None, base=None, start=None, span=None, norm=1.0, chunks=None, dtype=jnp.float32):
    AUG = features + TILE
    scale = math.log2(math.e) * 4.0 / features
    packed = not isinstance(rows, tuple)
    outs = rows.shape[0] - AUG if packed else rows[1].shape[1]
    low, cols = (0, right.shape[1]) if span is None else span
    shape = (outs, cols) if chunks is None else (chunks, outs, cols // chunks)
    pieces, piece = (1, rows.shape[1]) if packed else (rows[1].shape[0], rows[1].shape[2])
    row_block = min(ROW_BLOCK, piece)
    col_block = min(COL_BLOCK, cols)

    def body(*refs):
        refs = list(refs)
        base_ref = None if base is None else refs.pop(0)
        start_ref = None if start is None else refs.pop(0)
        left_ref = refs.pop(0)
        vals_ref = left_ref if packed else refs.pop(0)
        right_ref = refs.pop(0)
        first_ref = None if acc is None else refs.pop(0)
        out_ref, acc_ref = refs
        begin = 0 if base is None else pl.multiple_of(base_ref[0], piece)
        acc_ref[...] = jnp.zeros_like(acc_ref)

        ones = jnp.ones((TILE, max(row_block, col_block)), jnp.bfloat16)
        shift = low if start is None else pl.multiple_of(start_ref[0], cols)

        def inner(left, col):
            cut = pl.ds(shift + col, col_block)
            right = jnp.concatenate(
                [right_ref[0:features, cut], ones[:, :col_block], right_ref[features:AUG, cut]], axis=0
            )
            return jnp.dot(left, right, preferred_element_type=jnp.float32)

        def finish(state):
            vals, col, value = state
            kernel = jnp.exp2(value * scale).astype(jnp.bfloat16)
            acc_ref[:, col : col + col_block] += jnp.dot(vals, kernel, preferred_element_type=jnp.float32)

        state = None
        for at in range(pieces):
            for row in range(0, piece, row_block):
                left = left_ref[0:AUG, pl.ds(begin + at * piece + row, row_block)]
                left = jnp.concatenate([left, ones[:, :row_block]], axis=0).T
                if packed:
                    vals = vals_ref[AUG : AUG + outs, row : row + row_block]
                else:
                    vals = vals_ref[at, :, row : row + row_block]
                for col in range(0, cols, col_block):
                    value = inner(left, col)
                    if state is not None:
                        finish(state)
                    state = (vals, col, value)
        finish(state)

        width = cols if chunks is None else cols // chunks
        for at in range(cols // width):
            cut = slice(at * width, (at + 1) * width)
            total = acc_ref[:, cut]
            if norm != 1.0:
                total = total * norm
            if first_ref is not None:
                total = total + first_ref[:, low + at * width : low + (at + 1) * width]
            if chunks is None:
                out_ref[...] = total.astype(dtype)
            else:
                out_ref[at] = total.astype(dtype)

    vmem = pl.BlockSpec(memory_space=pltpu.VMEM)
    args = ([rows] if packed else list(rows)) + [right] + ([] if acc is None else [acc])
    specs = [vmem] * len(args)
    scalars = [value for value in (base, start) if value is not None]
    args = scalars + args
    specs = [pl.BlockSpec(memory_space=pltpu.SMEM)] * len(scalars) + specs
    count = pieces * piece
    return pl.pallas_call(
        body,
        in_specs=specs,
        out_specs=vmem,
        out_shape=jax.ShapeDtypeStruct(shape, dtype),
        scratch_shapes=[pltpu.VMEM((outs, cols), jnp.float32)],
        cost_estimate=pl.CostEstimate(
            flops=2 * count * cols * (AUG + outs), transcendentals=count * cols, bytes_accessed=2**21
        ),
    )(*args)


def source_group(dp_at, group_at, groups):
    if groups == 4:
        return ((0, 2, 1, 3), (1, 3, 0, 2), (2, 0, 3, 1), (3, 1, 2, 0))[dp_at][group_at]
    return (dp_at + group_at) % groups


def solution(mesh):
    dp_size = mesh.shape["dp"]
    cen_size = mesh.shape["centers"]
    pairs = cen_size // 2
    members = cen_size // dp_size
    swap = [(at, at ^ 1) for at in range(cen_size)]
    pair_groups = [[2 * at + core for at in range(pairs)] for core in range(2)]
    fetch = [
        (d * cen_size + source_group(d, g, dp_size) * members + m, d * cen_size + g * members + m)
        for d in range(dp_size)
        for g in range(dp_size)
        for m in range(members)
    ]

    def on_device(points, centers, coef):
        features = points.shape[1]
        local_pts = points.shape[0]
        half_pts = local_pts // 2
        total_pts = local_pts * dp_size
        core = lax.axis_index("centers") % 2
        own_base = (core * half_pts).astype(jnp.int32).reshape(1)

        pack, pts = prepare((centers.T, points.T), (coef.T, None))
        partner = lax.ppermute(pack, "centers", swap)
        fetched = lax.ppermute(pack, ("dp", "centers"), fetch)

        own_cols = dict(features=features, start=own_base, span=(0, half_pts))
        mine = product(pack, pts, **own_cols)
        partner, mine = lax.optimization_barrier((partner, mine))
        parts = product(partner, pts, acc=mine, chunks=pairs, dtype=jnp.bfloat16, **own_cols)
        others = [fetched]
        for step in range(1, members):
            ring = [
                (g * members + (m + step) % members, g * members + m)
                for g in range(dp_size)
                for m in range(members)
            ]
            others.append(lax.ppermute(fetched, "centers", ring))

        parts, others[0] = lax.optimization_barrier((parts, others[0]))
        regular = product(others[0], pack, features)
        parts = lax.all_to_all(parts, "centers", 0, 0, axis_index_groups=pair_groups)
        parts, regular = lax.optimization_barrier((parts, regular))
        shared = jnp.sum(parts.astype(jnp.float32), axis=0).astype(jnp.bfloat16)
        spread = jnp.broadcast_to(shared[None], (pairs,) + shared.shape)
        spread, regular = lax.optimization_barrier((spread, regular))
        first = lax.all_to_all(spread, "centers", 0, 0, axis_index_groups=pair_groups)
        for other in others[1:]:
            regular = product(other, pack, features, regular)
        first, regular = lax.optimization_barrier((first, regular))
        second = lax.ppermute(first, "centers", swap)

        norm = 1.0 / math.sqrt(total_pts)
        acc = product((pts, first), pack, features, regular, own_base, norm=norm)
        second, acc = lax.optimization_barrier((second, acc))
        half_cols = centers.shape[0] // 2
        rows = (pts, second)
        back_a = product(
            rows, pack, features, acc, half_pts - own_base, None, (0, half_cols), norm, dp_size
        )
        sums_a = scatter_sum(back_a)
        back_b = product(
            rows, pack, features, acc, half_pts - own_base, None, (half_cols, half_cols), norm, dp_size
        )
        sums_a, back_b = lax.optimization_barrier((sums_a, back_b))
        sum_a = sum(sums_a[1:], sums_a[0])
        sum_b = jnp.sum(lax.all_to_all(back_b, "dp", 0, 0), axis=0)
        both = jnp.stack([sum_a, sum_b])
        spread = jnp.broadcast_to(both[None], (dp_size,) + both.shape)
        whole = lax.all_to_all(spread, "dp", 0, 0)
        return whole.transpose(1, 0, 3, 2).reshape(centers.shape[0], coef.shape[1])

    def scatter_sum(parts):
        at = lax.axis_index("dp")
        pick = lambda step: lax.dynamic_index_in_dim(parts, (at + step) % dp_size, 0, keepdims=False)
        got = [pick(0)]
        for step in range(1, dp_size):
            ring = [(d, (d + step) % dp_size) for d in range(dp_size)]
            got.append(lax.ppermute(pick(step), "dp", ring))
        return got

    in_specs = (P("dp", None), P("centers", None), P("centers", None))

    return jax.shard_map(on_device, mesh=mesh, in_specs=in_specs, out_specs=P("centers", None), check_vma=False)
```

time: 193 us -> 87 us (0.45)
  waiting for transfers between devices: 105 us -> 10.3 us
  matrix products: 49 us -> 0 us
  Pallas kernels: 0 us -> 38.8 us
  starting transfers between devices: 0.12 us -> 21.1 us
  between operations: 13.2 us -> 0.11 us
  blocking collectives: 16.8 us -> 9.53 us
  other arithmetic: 4.13 us -> 0.2 us
    dot_general x10 -> x0, matrix products: 49 us -> none  [the longest x4 17.6 us: kernel_block(): lax.dot_general(left_pts, right_pts, (((1,), (1,)), ((), ())), preferred_...]
    psum x1 -> x0, waiting for transfers between devices: 44.9 us -> none  [on_device(): return lax.psum(back + placed, 'dp')]
    pallas_call x0 -> x8, Pallas kernels: none -> 38.8 us  [the longest x7 36.7 us: product(): pl.pallas_call(body, in_specs=specs, out_specs=vmem, out_shape=jax.ShapeD...]
    reduce_scatter x1 -> x0, waiting for transfers between devices: 31.9 us -> none  [on_device(): lax.psum_scatter(forward_part.astype(jnp.bfloat16), 'centers', scatter_di...]
    all_gather x2 -> x0, waiting for transfers between devices: 26.5 us -> none  [the longest x1 26.4 us: on_device(): piece_coef = lax.all_gather(coef, 'centers', axis=0, tiled=True)]
    all_gather x1 -> x0, blocking collectives: 16.8 us -> none  [on_device(): forward = lax.all_gather(shared, 'centers', axis=0, tiled=True)]
    all_to_all x0 -> x3, starting transfers between devices: none -> 13.1 us  [the longest x1 6.08 us: on_device(): lax.all_to_all(parts, 'centers', 0, 0, axis_index_groups=pair_groups)]
    all_to_all x0 -> x3, waiting for transfers between devices: none -> 10.3 us  [the longest x1 5.26 us: on_device(): sum_b = jnp.sum(lax.all_to_all(back_b, 'dp', 0, 0), axis=0)]
  transfers between devices with their start and end apart: 4 -> 10, of which waited for: 3 -> 3; matrix products, arithmetic and copies ran while one was open for 6% -> 1% of each run, Pallas kernels for 0% -> 38%
where the time goes in v1:
time: 87 us; the launch traced here: 86.3 us
  Pallas kernels  38.8 us (45%)
  starting transfers between devices  21.1 us (24%)
  waiting for transfers between devices  10.3 us (12%)
  blocking collectives  9.53 us (11%)
  local copies, waits for them, and re-layouts  6.31 us (7%)
    pallas_call x7, Pallas kernels, product(): pl.pallas_call(body, in_specs=specs, out_specs=vmem, out_shape=jax.ShapeD...  36.7 us
    all_to_all x1, blocking collectives, on_device(): whole = lax.all_to_all(spread, 'dp', 0, 0)  9.53 us
    all_to_all x1, starting transfers between devices, on_device(): lax.all_to_all(parts, 'centers', 0, 0, axis_index_groups=pair_groups)  6.08 us
    ppermute x3, starting transfers between devices, scatter_sum(): got.append(lax.ppermute(pick(step), 'dp', ring))  5.82 us
    all_to_all x1, waiting for transfers between devices, on_device(): sum_b = jnp.sum(lax.all_to_all(back_b, 'dp', 0, 0), axis=0)  5.26 us
    all_to_all x1, waiting for transfers between devices, on_device(): lax.all_to_all(parts, 'centers', 0, 0, axis_index_groups=pair_groups)  3.68 us
    all_to_all x1, starting transfers between devices, on_device(): lax.all_to_all(spread, 'centers', 0, 0, axis_index_groups=pair_groups)  3.58 us
    all_to_all x1, starting transfers between devices, on_device(): sum_b = jnp.sum(lax.all_to_all(back_b, 'dp', 0, 0), axis=0)  3.42 us
  transfers between devices with their start and end apart: 10, of which 3 were waited for; matrix products, arithmetic and copies ran while one was open for 1% of the time, Pallas kernels for 38%

profile of v1, /device:TPU:0, one launch (start us, length us, event | category | flops | bytes accessed | tf_op | source)
XLA Modules:
  0.0 86.3 jit_solution(3974797879992152183)
XLA Ops:
  0.0 2.1 %shard_map.37 = (bf16[112,2048]{1,0:T(8,128)(2,1)}, bf16[48,4096]{1,0:T(8,128)(2,1)}) custom-call(bf16[32,2048]{1,0:T(8,128)(2,1)} %bitcast.20, bf16[32,4096]{1,0:T(8,128)(2,1)} %bitcast.18, bf16[64,2048]{1,0:T(8,128)(2,1)} %bitcast.19), custom_call_target="tpu_custom_call" | custom-call | tf_op jit(solution)/shard_map/pallas_call | solution.py:41
  2.1 0.5 collective-permute-start
  2.6 1.7 %collective-permute-start.1 = (bf16[112,2048]{1,0:T(8,128)(2,1)}, bf16[112,2048]{1,0:T(8,128)(2,1)S(1)}, u32[]{:S(2)}, u32[]{:S(2)}) collective-permute-start(bf16[112,2048]{1,0:T(8,128)(2,1)} %get-tuple-element.25.refs_1_.refs_3_), channel_id=1, source_target_pairs={{0,0},{1,1},{4,2},{5,3},{2,4},{3,5},{6,6},{7,7},{10,8},{11,9},{14,... | collective-permute-start | bytes 1376264 | tf_op jit(solution)/shard_map/ppermute | solution.py:163
  4.3 5.6 %shard_map.38.refs_3_ = f32[64,2048]{1,0:T(8,128)} custom-call(s32[1]{0:T(128)} %bitcast.refs_0_, bf16[112,2048]{1,0:T(8,128)(2,1)} %get-tuple-element.25.refs_1_.refs_3_, bf16[48,4096]{1,0:T(8,128)(2,1)} %get-tuple-element.24.refs_2_.refs_1_), custom_call_target="tpu_custom_call" | custom-call | flops 939524096 | bytes 2097152 | tf_op jit(solution)/shard_map/pallas_call | solution.py:121
  9.9 0.0 collective-permute-done.refs_1_
  9.9 0.0 copy-start.2
  9.9 0.8 copy-done.2
  10.7 5.7 %shard_map.39 = bf16[4,64,512]{2,1,0:T(8,128)(2,1)} custom-call(s32[1]{0:T(128)} %bitcast.refs_0_, bf16[112,2048]{1,0:T(8,128)(2,1)} %copy-done.2, bf16[48,4096]{1,0:T(8,128)(2,1)} %get-tuple-element.24.refs_2_.refs_1_, f32[64,2048]{1,0:T(8,128)} %shard_map.38.refs_3_), custom_call_target="tpu_custom_call" | custom-call | flops 939524096 | bytes 2097152 | tf_op jit(solution)/shard_map/pallas_call | solution.py:121
  16.4 0.0 collective-permute-done.1.refs_0_
  16.4 0.0 copy-start.1
  16.4 6.1 %all-to-all-start = ((bf16[4,64,512]{2,1,0:T(8,128)(2,1)}), bf16[4,64,512]{2,1,0:T(8,128)(2,1)S(1)}, u32[]{:S(2)}, u32[]{:S(2)}) async-start(bf16[4,64,512]{2,1,0:T(8,128)(2,1)} %shard_map.39), calls=%async_computation | async-start | bytes 524288 | tf_op jit(solution)/shard_map/all_to_all | solution.py:180
  22.5 0.0 collective-permute-start.2
  22.5 0.0 copy-done.1
  22.5 5.6 %shard_map.40.refs_2_ = f32[64,2048]{1,0:T(8,128)} custom-call(bf16[112,2048]{1,0:T(8,128)(2,1)} %copy-done.1, bf16[112,2048]{1,0:T(8,128)(2,1)} %get-tuple-element.25.refs_1_.refs_3_), custom_call_target="tpu_custom_call" | custom-call | flops 939524096 | bytes 2097152 | tf_op jit(solution)/shard_map/pallas_call | solution.py:121
  28.1 3.7 %all-to-all-done = bf16[4,64,512]{2,1,0:T(8,128)(2,1)S(1)} async-done(((bf16[4,64,512]{2,1,0:T(8,128)(2,1)}), bf16[4,64,512]{2,1,0:T(8,128)(2,1)S(1)}, u32[]{:S(2)}, u32[]{:S(2)}) %all-to-all-start) | async-done | bytes 262176 | tf_op jit(solution)/shard_map/all_to_all | solution.py:180
  31.8 0.7 broadcast_in_dim.4
  32.6 3.6 %all-to-all-start.1 = ((bf16[4,64,512]{2,1,0:T(8,128)(2,1)}), bf16[4,64,512]{2,1,0:T(8,128)(2,1)S(1)}, u32[]{:S(2)}, u32[]{:S(2)}) async-start(bf16[4,64,512]{2,1,0:T(8,128)(2,1)} %broadcast_in_dim.4), calls=%async_computation.1 | async-start | bytes 524288 | tf_op jit(solution)/shard_map/all_to_all | solution.py:185
  36.2 0.0 collective-permute-done.2.refs_0_
  36.2 0.0 copy-start.3
  36.2 0.8 copy-done.3
  37.0 5.8 %shard_map.41.refs_4_ = f32[64,2048]{1,0:T(8,128)} custom-call(bf16[112,2048]{1,0:T(8,128)(2,1)} %copy-done.3, bf16[112,2048]{1,0:T(8,128)(2,1)} %get-tuple-element.25.refs_1_.refs_3_, f32[64,2048]{1,0:T(8,128)} %shard_map.40.refs_2_), custom_call_target="tpu_custom_call" | custom-call | flops 939524096 | bytes 2097152 | tf_op jit(solution)/shard_map/pallas_call | solution.py:121
  42.8 1.4 %all-to-all-done.1.refs_2_ = bf16[4,64,512]{2,1,0:T(8,128)(2,1)S(1)} async-done(((bf16[4,64,512]{2,1,0:T(8,128)(2,1)}), bf16[4,64,512]{2,1,0:T(8,128)(2,1)S(1)}, u32[]{:S(2)}, u32[]{:S(2)}) %all-to-all-start.1) | async-done | bytes 262176 | tf_op jit(solution)/shard_map/all_to_all | solution.py:185
  44.1 0.0 copy-start
  44.1 0.0 collective-permute-start.3
  44.2 0.7 copy-done
  44.9 5.9 %shard_map.42.refs_4_ = f32[64,2048]{1,0:T(8,128)} custom-call(s32[1]{0:T(128)} %bitcast.refs_0_, bf16[48,4096]{1,0:T(8,128)(2,1)} %get-tuple-element.24.refs_2_.refs_1_, bf16[4,64,512]{2,1,0:T(8,128)(2,1)} %copy-done, bf16[112,2048]{1,0:T(8,128)(2,1)} %get-tuple-element.25.refs_1_.refs_3_, f32[64,2048]{1,0:T(8,128)} %shard_map.41.refs_4_), custom_call_target="tpu_custom_call" | custom-call | flops 939524096 | bytes 2097152 | tf_op jit(solution)/shard_map/pallas_call | solution.py:121
  50.7 0.0 collective-permute-done.3.refs_2_
  50.7 0.0 copy-start.4
  50.7 0.7 copy-done.4
  51.4 4.0 %shard_map.43 = f32[4,64,256]{2,1,0:T(8,128)} custom-call(s32[1]{0:T(128)S(6)} %sub.4.refs_0_, bf16[48,4096]{1,0:T(8,128)(2,1)} %get-tuple-element.24.refs_2_.refs_1_, bf16[4,64,512]{2,1,0:T(8,128)(2,1)} %copy-done.4, bf16[112,2048]{1,0:T(8,128)(2,1)} %get-tuple-element.25.refs_1_.refs_3_, f32[64,2048]{1,0:T(8,128)} %shard_map.42.refs_4_), custom_call_target="tpu_custom_call" | custom-call | flops 469762048 | bytes 2097152 | tf_op jit(solution)/shard_map/pallas_call | solution.py:121
  55.5 1.0 %dynamic-slice_bitcast_fusion = (f32[64,256]{1,0:T(8,128)S(1)}, f32[64,256]{1,0:T(8,128)S(1)}, f32[64,256]{1,0:T(8,128)S(1)}, f32[64,256]{1,0:T(8,128)S(1)}) fusion(f32[4,64,256]{2,1,0:T(8,128)} %shard_map.43, s32[]{:T(128)S(6)} %select_n.44, s32[]{:T(128)S(6)} %select_n.42, s32[]{:T(128)S(6)} %select_n.40, s32[]{:T(128)S(6)} %select_n.38), kind=kLoop, calls=%fused_computation.2 | loop fusion | bytes 524304 | tf_op jit(solution)/shard_map/jit(dynamic_index_in_dim)/squeeze | solution.py:213
  56.4 1.7 %collective-permute-start.4 = (f32[64,256]{1,0:T(8,128)S(1)}, f32[64,256]{1,0:T(8,128)S(1)}, u32[]{:S(2)}, u32[]{:S(2)}) collective-permute-start(f32[64,256]{1,0:T(8,128)S(1)} %get-tuple-element.45), channel_id=1, source_target_pairs={{0,8},{8,16},{16,24},{24,0},{1,9},{9,17},{17,25},{25,1},{2,10},{10... | collective-permute-start | bytes 196616 | tf_op jit(solution)/shard_map/ppermute | solution.py:217
  58.1 3.7 %collective-permute-start.5 = (f32[64,256]{1,0:T(8,128)S(1)}, f32[64,256]{1,0:T(8,128)S(1)}, u32[]{:S(2)}, u32[]{:S(2)}) collective-permute-start(f32[64,256]{1,0:T(8,128)S(1)} %get-tuple-element.44), channel_id=1, source_target_pairs={{0,16},{8,24},{16,0},{24,8},{1,17},{9,25},{17,1},{25,9},{2,18},{10... | collective-permute-start | bytes 196616 | tf_op jit(solution)/shard_map/ppermute | solution.py:217
  61.9 0.3 collective-permute-start.6
  62.2 4.0 %shard_map.44 = f32[4,64,256]{2,1,0:T(8,128)} custom-call(s32[1]{0:T(128)S(6)} %sub.4.refs_0_, bf16[48,4096]{1,0:T(8,128)(2,1)} %get-tuple-element.24.refs_2_.refs_1_, bf16[4,64,512]{2,1,0:T(8,128)(2,1)} %copy-done.4, bf16[112,2048]{1,0:T(8,128)(2,1)} %get-tuple-element.25.refs_1_.refs_3_, f32[64,2048]{1,0:T(8,128)} %shard_map.42.refs_4_), custom_call_target="tpu_custom_call" | custom-call | flops 469762048 | bytes 2097152 | tf_op jit(solution)/shard_map/pallas_call | solution.py:121
  66.3 0.0 collective-permute-done.4
  66.3 0.0 collective-permute-done.5
  66.3 0.0 collective-permute-done.6
  66.3 3.4 %all-to-all-start.2 = ((f32[4,64,256]{2,1,0:T(8,128)}), f32[4,64,256]{2,1,0:T(8,128)S(1)}, u32[]{:S(2)}, u32[]{:S(2)}) async-start(f32[4,64,256]{2,1,0:T(8,128)} %shard_map.44), calls=%async_computation.2 | async-start | bytes 524288 | tf_op jit(solution)/shard_map/all_to_all | solution.py:205
  69.8 5.3 %all-to-all-done.2 = f32[4,64,256]{2,1,0:T(8,128)S(1)} async-done(((f32[4,64,256]{2,1,0:T(8,128)}), f32[4,64,256]{2,1,0:T(8,128)S(1)}, u32[]{:S(2)}, u32[]{:S(2)}) %all-to-all-start.2) | async-done | bytes 262176 | tf_op jit(solution)/shard_map/all_to_all | solution.py:205
  75.1 0.1 copy.6
  75.1 0.1 pad_maximum_fusion
  75.3 0.1 broadcast_in_dim.5
  75.4 9.5 %all_to_all.20 = f32[4,2,64,256]{3,1,2,0:T(2,128)S(1)} all-to-all(f32[4,2,64,256]{3,1,2,0:T(2,128)S(1)} %broadcast_in_dim.5), channel_id=1, replica_groups=mesh['dp'=4,'centers'=8] {'dp'}, dimensions={0} | all-to-all | bytes 1048576 | tf_op jit(solution)/shard_map/all_to_all | solution.py:208
  84.9 0.3 copy.7
  85.3 1.1 %reshape.9 = f32[2048,64]{0,1:T(8,128)} reshape(f32[2,4,256,64]{2,1,0,3:T(4,128)S(1)} %copy.7) | data formatting | bytes 1048576 | tf_op jit(solution)/shard_map/reshape | solution.py:209
  (4 shorter events, 0.1 us)
Async XLA Ops:
  2.1 7.8 %collective-permute-start = (bf16[112,2048]{1,0:T(8,128)(2,1)}, bf16[112,2048]{1,0:T(8,128)(2,1)S(1)}, u32[]{:S(2)}, u32[]{:S(2)}) collective-permute-start(bf16[112,2048]{1,0:T(8,128)(2,1)} %get-tuple-element.25.refs_1_.refs_3_), channel_id=1, source_target_pairs={{0,1},{1,0},{2,3},{3,2},{4,5},{5,4},{6,7},{7,6},{8,9},{9,8},{10,11... | collective-permute-start | bytes 1376264 | tf_op jit(solution)/shard_map/ppermute | solution.py:162
  2.6 13.8 %collective-permute-start.1 = (bf16[112,2048]{1,0:T(8,128)(2,1)}, bf16[112,2048]{1,0:T(8,128)(2,1)S(1)}, u32[]{:S(2)}, u32[]{:S(2)}) collective-permute-start(bf16[112,2048]{1,0:T(8,128)(2,1)} %get-tuple-element.25.refs_1_.refs_3_), channel_id=1, source_target_pairs={{0,0},{1,1},{4,2},{5,3},{2,4},{3,5},{6,6},{7,7},{10,8},{11,9},{14,... | collective-permute-start | bytes 1376264 | tf_op jit(solution)/shard_map/ppermute | solution.py:163
  9.9 0.8 copy-start.2
  16.4 6.1 %copy-start.1 = (bf16[112,2048]{1,0:T(8,128)(2,1)}, bf16[112,2048]{1,0:T(8,128)(2,1)S(1)}, u32[]{:S(2)}) copy-start(bf16[112,2048]{1,0:T(8,128)(2,1)S(1)} %collective-permute-done.1.refs_0_) | copy-start | bytes 1376260
  16.4 15.4 %all-to-all-start = ((bf16[4,64,512]{2,1,0:T(8,128)(2,1)}), bf16[4,64,512]{2,1,0:T(8,128)(2,1)S(1)}, u32[]{:S(2)}, u32[]{:S(2)}) async-start(bf16[4,64,512]{2,1,0:T(8,128)(2,1)} %shard_map.39), calls=%async_computation | async-start | bytes 524288 | tf_op jit(solution)/shard_map/all_to_all | solution.py:180
  22.5 13.7 %collective-permute-start.2 = (bf16[112,2048]{1,0:T(8,128)(2,1)S(1)}, bf16[112,2048]{1,0:T(8,128)(2,1)S(1)}, u32[]{:S(2)}, u32[]{:S(2)}) collective-permute-start(bf16[112,2048]{1,0:T(8,128)(2,1)S(1)} %collective-permute-done.1.refs_0_), channel_id=1, source_target_pairs={{1,0},{0,1},{3,2},{2,3},{5,4},{4,5},{7,6},{6,7},{9,8},{8,9},{11,10... | collective-permute-start | bytes 1376264 | tf_op jit(solution)/shard_map/ppermute | solution.py:176
  32.6 11.6 %all-to-all-start.1 = ((bf16[4,64,512]{2,1,0:T(8,128)(2,1)}), bf16[4,64,512]{2,1,0:T(8,128)(2,1)S(1)}, u32[]{:S(2)}, u32[]{:S(2)}) async-start(bf16[4,64,512]{2,1,0:T(8,128)(2,1)} %broadcast_in_dim.4), calls=%async_computation.1 | async-start | bytes 524288 | tf_op jit(solution)/shard_map/all_to_all | solution.py:185
  36.2 0.8 copy-start.3
  44.1 0.7 copy-start
  44.1 6.6 %collective-permute-start.3 = (bf16[4,64,512]{2,1,0:T(8,128)(2,1)S(1)}, bf16[4,64,512]{2,1,0:T(8,128)(2,1)S(1)}, u32[]{:S(2)}, u32[]{:S(2)}) collective-permute-start(bf16[4,64,512]{2,1,0:T(8,128)(2,1)S(1)} %all-to-all-done.1.refs_2_), channel_id=1, source_target_pairs={{0,1},{1,0},{2,3},{3,2},{4,5},{5,4},{6,7},{7,6},{8,9},{9,8},{10,11... | collective-permute-start | bytes 786440 | tf_op jit(solution)/shard_map/ppermute | solution.py:189
  50.7 0.7 copy-start.4
  56.4 9.9 %collective-permute-start.4 = (f32[64,256]{1,0:T(8,128)S(1)}, f32[64,256]{1,0:T(8,128)S(1)}, u32[]{:S(2)}, u32[]{:S(2)}) collective-permute-start(f32[64,256]{1,0:T(8,128)S(1)} %get-tuple-element.45), channel_id=1, source_target_pairs={{0,8},{8,16},{16,24},{24,0},{1,9},{9,17},{17,25},{25,1},{2,10},{10... | collective-permute-start | bytes 196616 | tf_op jit(solution)/shard_map/ppermute | solution.py:217
  58.1 8.1 %collective-permute-start.5 = (f32[64,256]{1,0:T(8,128)S(1)}, f32[64,256]{1,0:T(8,128)S(1)}, u32[]{:S(2)}, u32[]{:S(2)}) collective-permute-start(f32[64,256]{1,0:T(8,128)S(1)} %get-tuple-element.44), channel_id=1, source_target_pairs={{0,16},{8,24},{16,0},{24,8},{1,17},{9,25},{17,1},{25,9},{2,18},{10... | collective-permute-start | bytes 196616 | tf_op jit(solution)/shard_map/ppermute | solution.py:217
  61.9 4.4 %collective-permute-start.6 = (f32[64,256]{1,0:T(8,128)S(1)}, f32[64,256]{1,0:T(8,128)S(1)}, u32[]{:S(2)}, u32[]{:S(2)}) collective-permute-start(f32[64,256]{1,0:T(8,128)S(1)} %get-tuple-element.43), channel_id=1, source_target_pairs={{0,24},{8,0},{16,8},{24,16},{1,25},{9,1},{17,9},{25,17},{2,26},{10... | collective-permute-start | bytes 196616 | tf_op jit(solution)/shard_map/ppermute | solution.py:217
  66.3 8.8 %all-to-all-start.2 = ((f32[4,64,256]{2,1,0:T(8,128)}), f32[4,64,256]{2,1,0:T(8,128)S(1)}, u32[]{:S(2)}, u32[]{:S(2)}) async-start(f32[4,64,256]{2,1,0:T(8,128)} %shard_map.44), calls=%async_computation.2 | async-start | bytes 524288 | tf_op jit(solution)/shard_map/all_to_all | solution.py:205

commit v2 on v1

--- a/solution.py
+++ b/solution.py
@@ -40,7 +40,7 @@
     ]
     return pl.pallas_call(
         body,
-        out_shape=[jax.ShapeDtypeStruct(shape, jnp.bfloat16) for shape in shapes],
+        out_shape=[pltpu.VMEM(shape, jnp.bfloat16) for shape in shapes],
     )(*feats, *[values[at] for at in present])
 
 
@@ -114,6 +114,7 @@
     vmem = pl.BlockSpec(memory_space=pltpu.VMEM)
     args = ([rows] if packed else list(rows)) + [right] + ([] if acc is None else [acc])
     specs = [vmem] * len(args)
+    args = [pltpu.with_memory_space_constraint(arg, pltpu.VMEM) for arg in args]
     scalars = [value for value in (base, start) if value is not None]
     args = scalars + args
     specs = [pl.BlockSpec(memory_space=pltpu.SMEM)] * len(scalars) + specs
@@ -122,7 +123,7 @@
         body,
         in_specs=specs,
         out_specs=vmem,
-        out_shape=jax.ShapeDtypeStruct(shape, dtype),
+        out_shape=pltpu.VMEM(shape, dtype),
         scratch_shapes=[pltpu.VMEM((outs, cols), jnp.float32)],
         cost_estimate=pl.CostEstimate(
             flops=2 * count * cols * (AUG + outs), transcendentals=count * cols, bytes_accessed=2**21

time: 87 us -> 77.8 us (0.89)
  Pallas kernels: 38.8 us -> 24.9 us
  starting transfers between devices: 21.1 us -> 25.5 us
  waiting for transfers between devices: 10.3 us -> 14.5 us
  local copies, waits for them, and re-layouts: 6.31 us -> 2.42 us
    pallas_call x8, Pallas kernels: 38.8 us -> 24.9 us  [the longest x7 23.7 us: product(): pl.pallas_call(body, in_specs=specs, out_specs=vmem, out_shape=pltpu.VMEM...]
    all_to_all x1, starting transfers between devices: 6.08 us -> 10.8 us  [on_device(): lax.all_to_all(parts, 'centers', 0, 0, axis_index_groups=pair_groups)]
    unnamed x10 -> x4, local copies, waits for them, and re-layouts: 2.96 us -> 0.01 us
    all_to_all x1, waiting for transfers between devices: 1.38 us -> 3.16 us  [on_device(): lax.all_to_all(spread, 'centers', 0, 0, axis_index_groups=pair_groups)]
    all_to_all x1, waiting for transfers between devices: 3.68 us -> 4.99 us  [on_device(): lax.all_to_all(parts, 'centers', 0, 0, axis_index_groups=pair_groups)]
    ppermute x3, waiting for transfers between devices: 0.01 us -> 1.09 us  [scatter_sum(): got.append(lax.ppermute(pick(step), 'dp', ring))]
    ppermute x1, starting transfers between devices: 1.66 us -> 0.68 us  [on_device(): fetched = lax.ppermute(pack, ('dp', 'centers'), fetch)]
    squeeze x1, local copies, waits for them, and re-layouts: 0.95 us -> 0.03 us  [scatter_sum(): lax.dynamic_index_in_dim(parts, (at + step) % dp_size, 0, keepdims=False)]
  transfers between devices with their start and end apart: 10 -> 10, of which waited for: 3 -> 5; matrix products, arithmetic and copies ran while one was open for 1% -> 1% of each run, Pallas kernels for 38% -> 28%
where the time goes in v2:
time: 77.8 us; the launch traced here: 77.3 us
  starting transfers between devices  25.5 us (33%)
  Pallas kernels  24.9 us (32%)
  waiting for transfers between devices  14.5 us (19%)
  blocking collectives  9.63 us (12%)
  local copies, waits for them, and re-layouts  2.42 us (3%)
    pallas_call x7, Pallas kernels, product(): pl.pallas_call(body, in_specs=specs, out_specs=vmem, out_shape=pltpu.VMEM...  23.7 us
    all_to_all x1, starting transfers between devices, on_device(): lax.all_to_all(parts, 'centers', 0, 0, axis_index_groups=pair_groups)  10.8 us
    all_to_all x1, blocking collectives, on_device(): whole = lax.all_to_all(spread, 'dp', 0, 0)  9.63 us
    ppermute x3, starting transfers between devices, scatter_sum(): got.append(lax.ppermute(pick(step), 'dp', ring))  6.41 us
    all_to_all x1, waiting for transfers between devices, on_device(): sum_b = jnp.sum(lax.all_to_all(back_b, 'dp', 0, 0), axis=0)  5.26 us
    all_to_all x1, waiting for transfers between devices, on_device(): lax.all_to_all(parts, 'centers', 0, 0, axis_index_groups=pair_groups)  4.99 us
    all_to_all x1, starting transfers between devices, on_device(): lax.all_to_all(spread, 'centers', 0, 0, axis_index_groups=pair_groups)  3.58 us
    all_to_all x1, starting transfers between devices, on_device(): sum_b = jnp.sum(lax.all_to_all(back_b, 'dp', 0, 0), axis=0)  3.41 us
  transfers between devices with their start and end apart: 10, of which 5 were waited for; matrix products, arithmetic and copies ran while one was open for 1% of the time, Pallas kernels for 28%

profile of v2, /device:TPU:0, one launch (start us, length us, event | category | flops | bytes accessed | tf_op | source)
XLA Modules:
  0.0 77.3 jit_solution(15029794292512986204)
XLA Ops:
  0.0 1.3 %shard_map.37 = (bf16[112,2048]{1,0:T(8,128)(2,1)S(1)}, bf16[48,4096]{1,0:T(8,128)(2,1)S(1)}) custom-call(bf16[32,2048]{1,0:T(8,128)(2,1)} %bitcast.20, bf16[32,4096]{1,0:T(8,128)(2,1)} %bitcast.18, bf16[64,2048]{1,0:T(8,128)(2,1)} %bitcast.19), custom_call_target="tpu_custom_call" | custom-call | tf_op jit(solution)/shard_map/pallas_call | solution.py:41
  1.3 0.0 copy-start
  1.3 0.6 collective-permute-start
  1.8 0.7 collective-permute-start.1
  2.5 3.7 %shard_map.38.refs_3_ = f32[64,2048]{1,0:T(8,128)S(1)} custom-call(s32[1]{0:T(128)} %bitcast.refs_0_, bf16[112,2048]{1,0:T(8,128)(2,1)S(1)} %get-tuple-element.25.refs_1_.refs_3_, bf16[48,4096]{1,0:T(8,128)(2,1)S(1)} %get-tuple-element.24.refs_2_.refs_1_), custom_call_target="tpu_custom_call" | custom-call | flops 939524096 | bytes 2097152 | tf_op jit(solution)/shard_map/pallas_call | solution.py:122
  6.2 0.0 collective-permute-done.refs_1_
  6.2 0.0 copy-done
  6.2 4.4 %shard_map.39 = bf16[4,64,512]{2,1,0:T(8,128)(2,1)} custom-call(s32[1]{0:T(128)} %bitcast.refs_0_, bf16[112,2048]{1,0:T(8,128)(2,1)S(1)} %collective-permute-done.refs_1_, bf16[48,4096]{1,0:T(8,128)(2,1)S(1)} %get-tuple-element.24.refs_2_.refs_1_, f32[64,2048]{1,0:T(8,128)S(1)} %shard_map.38.refs_3_), custom_call_target="tpu_custom_call" | custom-call | flops 939524096 | bytes 2097152 | tf_op jit(solution)/shard_map/pallas_call | solution.py:122
  10.6 0.0 collective-permute-done.1.refs_0_
  10.6 10.8 %all-to-all-start = ((bf16[4,64,512]{2,1,0:T(8,128)(2,1)}), bf16[4,64,512]{2,1,0:T(8,128)(2,1)S(1)}, u32[]{:S(2)}, u32[]{:S(2)}) async-start(bf16[4,64,512]{2,1,0:T(8,128)(2,1)} %shard_map.39), calls=%async_computation | async-start | bytes 524288 | tf_op jit(solution)/shard_map/all_to_all | solution.py:181
  21.5 0.0 collective-permute-start.2
  21.5 3.7 %shard_map.40.refs_2_ = f32[64,2048]{1,0:T(8,128)S(1)} custom-call(bf16[112,2048]{1,0:T(8,128)(2,1)S(1)} %collective-permute-done.1.refs_0_, bf16[112,2048]{1,0:T(8,128)(2,1)S(1)} %get-tuple-element.25.refs_1_.refs_3_), custom_call_target="tpu_custom_call" | custom-call | flops 939524096 | bytes 2097152 | tf_op jit(solution)/shard_map/pallas_call | solution.py:122
  25.2 5.0 %all-to-all-done = bf16[4,64,512]{2,1,0:T(8,128)(2,1)S(1)} async-done(((bf16[4,64,512]{2,1,0:T(8,128)(2,1)}), bf16[4,64,512]{2,1,0:T(8,128)(2,1)S(1)}, u32[]{:S(2)}, u32[]{:S(2)}) %all-to-all-start) | async-done | bytes 262176 | tf_op jit(solution)/shard_map/all_to_all | solution.py:181
  30.2 0.7 broadcast_in_dim.4
  30.9 3.6 %all-to-all-start.1 = ((bf16[4,64,512]{2,1,0:T(8,128)(2,1)}), bf16[4,64,512]{2,1,0:T(8,128)(2,1)S(1)}, u32[]{:S(2)}, u32[]{:S(2)}) async-start(bf16[4,64,512]{2,1,0:T(8,128)(2,1)} %broadcast_in_dim.4), calls=%async_computation.1 | async-start | bytes 524288 | tf_op jit(solution)/shard_map/all_to_all | solution.py:186
  34.5 0.0 copy-start.1
  34.5 0.0 collective-permute-done.2.refs_0_
  34.5 3.7 %shard_map.41.refs_4_ = f32[64,2048]{1,0:T(8,128)S(1)} custom-call(bf16[112,2048]{1,0:T(8,128)(2,1)S(1)} %collective-permute-done.2.refs_0_, bf16[112,2048]{1,0:T(8,128)(2,1)S(1)} %get-tuple-element.25.refs_1_.refs_3_, f32[64,2048]{1,0:T(8,128)S(1)} %shard_map.40.refs_2_), custom_call_target="tpu_custom_call" | custom-call | flops 939524096 | bytes 2097152 | tf_op jit(solution)/shard_map/pallas_call | solution.py:122
  38.2 3.2 %all-to-all-done.1.refs_2_ = bf16[4,64,512]{2,1,0:T(8,128)(2,1)S(1)} async-done(((bf16[4,64,512]{2,1,0:T(8,128)(2,1)}), bf16[4,64,512]{2,1,0:T(8,128)(2,1)S(1)}, u32[]{:S(2)}, u32[]{:S(2)}) %all-to-all-start.1) | async-done | bytes 262176 | tf_op jit(solution)/shard_map/all_to_all | solution.py:186
  41.4 0.0 collective-permute-start.3
  41.4 0.0 copy-done.1
  41.4 3.7 %shard_map.42.refs_4_ = f32[64,2048]{1,0:T(8,128)S(1)} custom-call(s32[1]{0:T(128)} %bitcast.refs_0_, bf16[48,4096]{1,0:T(8,128)(2,1)S(1)} %copy-done.1, bf16[4,64,512]{2,1,0:T(8,128)(2,1)S(1)} %all-to-all-done.1.refs_2_, bf16[112,2048]{1,0:T(8,128)(2,1)S(1)} %get-tuple-element.25.refs_1_.refs_3_, f32[64,2048]{1,0:T(8,128)S(1)} %shard_map.41.refs_4_), custom_call_target="tpu_custom_call" | custom-call | flops 939524096 | bytes 2097152 | tf_op jit(solution)/shard_map/pallas_call | solution.py:122
  45.1 0.0 collective-permute-done.3.refs_2_
  45.1 1.9 %shard_map.43 = f32[4,64,256]{2,1,0:T(8,128)S(1)} custom-call(s32[1]{0:T(128)S(6)} %sub.4.refs_0_, bf16[48,4096]{1,0:T(8,128)(2,1)S(1)} %copy-done.1, bf16[4,64,512]{2,1,0:T(8,128)(2,1)S(1)} %collective-permute-done.3.refs_2_, bf16[112,2048]{1,0:T(8,128)(2,1)S(1)} %get-tuple-element.25.refs_1_.refs_3_, f32[64,2048]{1,0:T(8,128)S(1)} %shard_map.42.refs_4_), custom_call_target="tpu_custom_call" | custom-call | flops 469762048 | bytes 2097152 | tf_op jit(solution)/shard_map/pallas_call | solution.py:122
  47.0 2.6 %collective-permute-start.4 = (f32[64,256]{1,0:T(8,128)S(1)}, f32[64,256]{1,0:T(8,128)S(1)}, u32[]{:S(2)}, u32[]{:S(2)}) collective-permute-start(f32[64,256]{1,0:T(8,128)S(1)} %get-tuple-element.45), channel_id=1, source_target_pairs={{0,8},{8,16},{16,24},{24,0},{1,9},{9,17},{17,25},{25,1},{2,10},{10... | collective-permute-start | bytes 196616 | tf_op jit(solution)/shard_map/ppermute | solution.py:218
  49.6 3.3 %collective-permute-start.5 = (f32[64,256]{1,0:T(8,128)S(1)}, f32[64,256]{1,0:T(8,128)S(1)}, u32[]{:S(2)}, u32[]{:S(2)}) collective-permute-start(f32[64,256]{1,0:T(8,128)S(1)} %get-tuple-element.44), channel_id=1, source_target_pairs={{0,16},{8,24},{16,0},{24,8},{1,17},{9,25},{17,1},{25,9},{2,18},{10... | collective-permute-start | bytes 196616 | tf_op jit(solution)/shard_map/ppermute | solution.py:218
  52.9 0.5 collective-permute-start.6
  53.4 2.6 %shard_map.44 = f32[4,64,256]{2,1,0:T(8,128)} custom-call(s32[1]{0:T(128)S(6)} %sub.4.refs_0_, bf16[48,4096]{1,0:T(8,128)(2,1)S(1)} %copy-done.1, bf16[4,64,512]{2,1,0:T(8,128)(2,1)S(1)} %collective-permute-done.3.refs_2_, bf16[112,2048]{1,0:T(8,128)(2,1)S(1)} %get-tuple-element.25.refs_1_.refs_3_, f32[64,2048]{1,0:T(8,128)S(1)} %shard_map.42.refs_4_), custom_call_target="tpu_custom_call" | custom-call | flops 469762048 | bytes 2097152 | tf_op jit(solution)/shard_map/pallas_call | solution.py:122
  56.1 0.0 collective-permute-done.4
  56.1 0.4 collective-permute-done.5
  56.5 0.7 collective-permute-done.6
  57.2 3.4 %all-to-all-start.2 = ((f32[4,64,256]{2,1,0:T(8,128)}), f32[4,64,256]{2,1,0:T(8,128)S(1)}, u32[]{:S(2)}, u32[]{:S(2)}) async-start(f32[4,64,256]{2,1,0:T(8,128)} %shard_map.44), calls=%async_computation.2 | async-start | bytes 524288 | tf_op jit(solution)/shard_map/all_to_all | solution.py:206
  60.7 5.3 %all-to-all-done.2 = f32[4,64,256]{2,1,0:T(8,128)S(1)} async-done(((f32[4,64,256]{2,1,0:T(8,128)}), f32[4,64,256]{2,1,0:T(8,128)S(1)}, u32[]{:S(2)}, u32[]{:S(2)}) %all-to-all-start.2) | async-done | bytes 262176 | tf_op jit(solution)/shard_map/all_to_all | solution.py:206
  66.0 0.1 copy.6
  66.0 0.1 pad_maximum_fusion
  66.2 0.1 broadcast_in_dim.5
  66.3 9.6 %all_to_all.20 = f32[4,2,64,256]{3,1,2,0:T(2,128)S(1)} all-to-all(f32[4,2,64,256]{3,1,2,0:T(2,128)S(1)} %broadcast_in_dim.5), channel_id=1, replica_groups=mesh['dp'=4,'centers'=8] {'dp'}, dimensions={0} | all-to-all | bytes 1048576 | tf_op jit(solution)/shard_map/all_to_all | solution.py:209
  75.9 0.3 copy.7
  76.3 1.1 %reshape.9 = f32[2048,64]{0,1:T(8,128)} reshape(f32[2,4,256,64]{2,1,0,3:T(4,128)S(1)} %copy.7) | data formatting | bytes 1048576 | tf_op jit(solution)/shard_map/reshape | solution.py:210
  (5 shorter events, 0.1 us)
Async XLA Ops:
  1.3 5.0 %copy-start = (bf16[48,4096]{1,0:T(8,128)(2,1)}, bf16[48,4096]{1,0:T(8,128)(2,1)S(1)}, u32[]{:S(2)}) copy-start(bf16[48,4096]{1,0:T(8,128)(2,1)S(1)} %get-tuple-element.24.refs_2_.refs_1_) | copy-start | bytes 1179652
  1.3 4.9 %collective-permute-start = (bf16[112,2048]{1,0:T(8,128)(2,1)S(1)}, bf16[112,2048]{1,0:T(8,128)(2,1)S(1)}, u32[]{:S(2)}, u32[]{:S(2)}) collective-permute-start(bf16[112,2048]{1,0:T(8,128)(2,1)S(1)} %get-tuple-element.25.refs_1_.refs_3_), channel_id=1, source_target_pairs={{0,1},{1,0},{2,3},{3,2},{4,5},{5,4},{6,7},{7,6},{8,9},{9,8},{10,11... | collective-permute-start | bytes 1376264 | tf_op jit(solution)/shard_map/ppermute | solution.py:163
  1.8 8.8 %collective-permute-start.1 = (bf16[112,2048]{1,0:T(8,128)(2,1)S(1)}, bf16[112,2048]{1,0:T(8,128)(2,1)S(1)}, u32[]{:S(2)}, u32[]{:S(2)}) collective-permute-start(bf16[112,2048]{1,0:T(8,128)(2,1)S(1)} %get-tuple-element.25.refs_1_.refs_3_), channel_id=1, source_target_pairs={{0,0},{1,1},{4,2},{5,3},{2,4},{3,5},{6,6},{7,7},{10,8},{11,9},{14,... | collective-permute-start | bytes 1376264 | tf_op jit(solution)/shard_map/ppermute | solution.py:164
  10.6 19.5 %all-to-all-start = ((bf16[4,64,512]{2,1,0:T(8,128)(2,1)}), bf16[4,64,512]{2,1,0:T(8,128)(2,1)S(1)}, u32[]{:S(2)}, u32[]{:S(2)}) async-start(bf16[4,64,512]{2,1,0:T(8,128)(2,1)} %shard_map.39), calls=%async_computation | async-start | bytes 524288 | tf_op jit(solution)/shard_map/all_to_all | solution.py:181
  21.5 13.0 %collective-permute-start.2 = (bf16[112,2048]{1,0:T(8,128)(2,1)S(1)}, bf16[112,2048]{1,0:T(8,128)(2,1)S(1)}, u32[]{:S(2)}, u32[]{:S(2)}) collective-permute-start(bf16[112,2048]{1,0:T(8,128)(2,1)S(1)} %collective-permute-done.1.refs_0_), channel_id=1, source_target_pairs={{1,0},{0,1},{3,2},{2,3},{5,4},{4,5},{7,6},{6,7},{9,8},{8,9},{11,10... | collective-permute-start | bytes 1376264 | tf_op jit(solution)/shard_map/ppermute | solution.py:177
  30.9 10.5 %all-to-all-start.1 = ((bf16[4,64,512]{2,1,0:T(8,128)(2,1)}), bf16[4,64,512]{2,1,0:T(8,128)(2,1)S(1)}, u32[]{:S(2)}, u32[]{:S(2)}) async-start(bf16[4,64,512]{2,1,0:T(8,128)(2,1)} %broadcast_in_dim.4), calls=%async_computation.1 | async-start | bytes 524288 | tf_op jit(solution)/shard_map/all_to_all | solution.py:186
  34.5 6.9 %copy-start.1 = (bf16[48,4096]{1,0:T(8,128)(2,1)S(1)}, bf16[48,4096]{1,0:T(8,128)(2,1)}, u32[]{:S(2)}) copy-start(bf16[48,4096]{1,0:T(8,128)(2,1)} %copy-done) | copy-start | bytes 1179652
  41.4 3.7 %collective-permute-start.3 = (bf16[4,64,512]{2,1,0:T(8,128)(2,1)S(1)}, bf16[4,64,512]{2,1,0:T(8,128)(2,1)S(1)}, u32[]{:S(2)}, u32[]{:S(2)}) collective-permute-start(bf16[4,64,512]{2,1,0:T(8,128)(2,1)S(1)} %all-to-all-done.1.refs_2_), channel_id=1, source_target_pairs={{0,1},{1,0},{2,3},{3,2},{4,5},{5,4},{6,7},{7,6},{8,9},{9,8},{10,11... | collective-permute-start | bytes 786440 | tf_op jit(solution)/shard_map/ppermute | solution.py:190
  47.0 9.1 %collective-permute-start.4 = (f32[64,256]{1,0:T(8,128)S(1)}, f32[64,256]{1,0:T(8,128)S(1)}, u32[]{:S(2)}, u32[]{:S(2)}) collective-permute-start(f32[64,256]{1,0:T(8,128)S(1)} %get-tuple-element.45), channel_id=1, source_target_pairs={{0,8},{8,16},{16,24},{24,0},{1,9},{9,17},{17,25},{25,1},{2,10},{10... | collective-permute-start | bytes 196616 | tf_op jit(solution)/shard_map/ppermute | solution.py:218
  49.6 6.9 %collective-permute-start.5 = (f32[64,256]{1,0:T(8,128)S(1)}, f32[64,256]{1,0:T(8,128)S(1)}, u32[]{:S(2)}, u32[]{:S(2)}) collective-permute-start(f32[64,256]{1,0:T(8,128)S(1)} %get-tuple-element.44), channel_id=1, source_target_pairs={{0,16},{8,24},{16,0},{24,8},{1,17},{9,25},{17,1},{25,9},{2,18},{10... | collective-permute-start | bytes 196616 | tf_op jit(solution)/shard_map/ppermute | solution.py:218
  52.9 4.3 %collective-permute-start.6 = (f32[64,256]{1,0:T(8,128)S(1)}, f32[64,256]{1,0:T(8,128)S(1)}, u32[]{:S(2)}, u32[]{:S(2)}) collective-permute-start(f32[64,256]{1,0:T(8,128)S(1)} %get-tuple-element.43), channel_id=1, source_target_pairs={{0,24},{8,0},{16,8},{24,16},{1,25},{9,1},{17,9},{25,17},{2,26},{10... | collective-permute-start | bytes 196616 | tf_op jit(solution)/shard_map/ppermute | solution.py:218
  57.2 8.8 %all-to-all-start.2 = ((f32[4,64,256]{2,1,0:T(8,128)}), f32[4,64,256]{2,1,0:T(8,128)S(1)}, u32[]{:S(2)}, u32[]{:S(2)}) async-start(f32[4,64,256]{2,1,0:T(8,128)} %shard_map.44), calls=%async_computation.2 | async-start | bytes 524288 | tf_op jit(solution)/shard_map/all_to_all | solution.py:206

commit v3 on v2

--- a/solution.py
+++ b/solution.py
@@ -176,9 +176,8 @@
             ]
             others.append(lax.ppermute(fetched, "centers", ring))
 
-        parts, others[0] = lax.optimization_barrier((parts, others[0]))
+        parts = lax.all_to_all(parts, "centers", 0, 0, axis_index_groups=pair_groups)
         regular = product(others[0], pack, features)
-        parts = lax.all_to_all(parts, "centers", 0, 0, axis_index_groups=pair_groups)
         parts, regular = lax.optimization_barrier((parts, regular))
         shared = jnp.sum(parts.astype(jnp.float32), axis=0).astype(jnp.bfloat16)
         spread = jnp.broadcast_to(shared[None], (pairs,) + shared.shape)
@@ -192,31 +191,12 @@
         norm = 1.0 / math.sqrt(total_pts)
         acc = product((pts, first), pack, features, regular, own_base, norm=norm)
         second, acc = lax.optimization_barrier((second, acc))
-        half_cols = centers.shape[0] // 2
         rows = (pts, second)
-        back_a = product(
-            rows, pack, features, acc, half_pts - own_base, None, (0, half_cols), norm, dp_size
-        )
-        sums_a = scatter_sum(back_a)
-        back_b = product(
-            rows, pack, features, acc, half_pts - own_base, None, (half_cols, half_cols), norm, dp_size
-        )
-        sums_a, back_b = lax.optimization_barrier((sums_a, back_b))
-        sum_a = sum(sums_a[1:], sums_a[0])
-        sum_b = jnp.sum(lax.all_to_all(back_b, "dp", 0, 0), axis=0)
-        both = jnp.stack([sum_a, sum_b])
-        spread = jnp.broadcast_to(both[None], (dp_size,) + both.shape)
+        back = product(rows, pack, features, acc, half_pts - own_base, norm=norm, chunks=dp_size)
+        summed = jnp.sum(lax.all_to_all(back, "dp", 0, 0), axis=0)
+        spread = jnp.broadcast_to(summed[None], (dp_size,) + summed.shape)
         whole = lax.all_to_all(spread, "dp", 0, 0)
-        return whole.transpose(1, 0, 3, 2).reshape(centers.shape[0], coef.shape[1])
-
-    def scatter_sum(parts):
-        at = lax.axis_index("dp")
-        pick = lambda step: lax.dynamic_index_in_dim(parts, (at + step) % dp_size, 0, keepdims=False)
-        got = [pick(0)]
-        for step in range(1, dp_size):
-            ring = [(d, (d + step) % dp_size) for d in range(dp_size)]
-            got.append(lax.ppermute(pick(step), "dp", ring))
-        return got
+        return whole.transpose(0, 2, 1).reshape(centers.shape[0], coef.shape[1])
 
     in_specs = (P("dp", None), P("centers", None), P("centers", None))
 

time: 77.8 us -> 72.3 us (0.929)
  blocking collectives: 9.63 us -> 24.2 us
  starting transfers between devices: 25.5 us -> 11.5 us
  waiting for transfers between devices: 14.5 us -> 10.5 us
  Pallas kernels: 24.9 us -> 24 us
  local copies, waits for them, and re-layouts: 2.42 us -> 1.62 us
    all_to_all x0 -> x1, blocking collectives: none -> 13.8 us  [on_device(): summed = jnp.sum(lax.all_to_all(back, 'dp', 0, 0), axis=0)]
    ppermute x3 -> x0, starting transfers between devices: 6.41 us -> none  [scatter_sum(): got.append(lax.ppermute(pick(step), 'dp', ring))]
    all_to_all x1 -> x0, waiting for transfers between devices: 5.26 us -> none  [on_device(): sum_b = jnp.sum(lax.all_to_all(back_b, 'dp', 0, 0), axis=0)]
    all_to_all x1, starting transfers between devices: 10.8 us -> 6.65 us  [on_device(): lax.all_to_all(parts, 'centers', 0, 0, axis_index_groups=pair_groups)]
    all_to_all x1 -> x0, starting transfers between devices: 3.41 us -> none  [on_device(): sum_b = jnp.sum(lax.all_to_all(back_b, 'dp', 0, 0), axis=0)]
    all_to_all x1, waiting for transfers between devices: 3.16 us -> 4.84 us  [on_device(): lax.all_to_all(spread, 'centers', 0, 0, axis_index_groups=pair_groups)]
    ppermute x3 -> x0, waiting for transfers between devices: 1.09 us -> none  [scatter_sum(): got.append(lax.ppermute(pick(step), 'dp', ring))]
    pallas_call x7 -> x6, Pallas kernels: 23.7 us -> 22.7 us  [product(): pl.pallas_call(body, in_specs=specs, out_specs=vmem, out_shape=pltpu.VMEM...]
  transfers between devices with their start and end apart: 10 -> 6, of which waited for: 5 -> 2; matrix products, arithmetic and copies ran while one was open for 1% -> 1% of each run, Pallas kernels for 28% -> 27%
where the time goes in v3:
time: 72.3 us; the launch traced here: 71.9 us
  blocking collectives  24.2 us (33%)
  Pallas kernels  24 us (33%)
  starting transfers between devices  11.5 us (16%)
  waiting for transfers between devices  10.5 us (15%)
  local copies, waits for them, and re-layouts  1.62 us (2%)
    pallas_call x6, Pallas kernels, product(): pl.pallas_call(body, in_specs=specs, out_specs=vmem, out_shape=pltpu.VMEM...  22.7 us
    all_to_all x1, blocking collectives, on_device(): summed = jnp.sum(lax.all_to_all(back, 'dp', 0, 0), axis=0)  13.8 us
    all_to_all x1, blocking collectives, on_device(): whole = lax.all_to_all(spread, 'dp', 0, 0)  10.4 us
    all_to_all x1, starting transfers between devices, on_device(): lax.all_to_all(parts, 'centers', 0, 0, axis_index_groups=pair_groups)  6.65 us
    all_to_all x1, waiting for transfers between devices, on_device(): lax.all_to_all(parts, 'centers', 0, 0, axis_index_groups=pair_groups)  5.6 us
    all_to_all x1, waiting for transfers between devices, on_device(): lax.all_to_all(spread, 'centers', 0, 0, axis_index_groups=pair_groups)  4.84 us
    all_to_all x1, starting transfers between devices, on_device(): lax.all_to_all(spread, 'centers', 0, 0, axis_index_groups=pair_groups)  3.58 us
  transfers between devices with their start and end apart: 6, of which 2 were waited for; matrix products, arithmetic and copies ran while one was open for 1% of the time, Pallas kernels for 27%

profile of v3, /device:TPU:0, one launch (start us, length us, event | category | flops | bytes accessed | tf_op | source)
XLA Modules:
  0.0 71.9 jit_solution(6862899932021612332)
XLA Ops:
  0.0 1.3 %shard_map.37 = (bf16[112,2048]{1,0:T(8,128)(2,1)S(1)}, bf16[48,4096]{1,0:T(8,128)(2,1)S(1)}) custom-call(bf16[32,2048]{1,0:T(8,128)(2,1)} %bitcast.10, bf16[32,4096]{1,0:T(8,128)(2,1)} %bitcast.8, bf16[64,2048]{1,0:T(8,128)(2,1)} %bitcast.9), custom_call_target="tpu_custom_call" | custom-call | tf_op jit(solution)/shard_map/pallas_call | solution.py:41
  1.3 0.0 copy-start
  1.3 0.6 collective-permute-start
  1.8 0.7 collective-permute-start.1
  2.5 3.7 %shard_map.38.refs_3_ = f32[64,2048]{1,0:T(8,128)S(1)} custom-call(s32[1]{0:T(128)} %bitcast.refs_0_, bf16[112,2048]{1,0:T(8,128)(2,1)S(1)} %get-tuple-element.18.refs_1_.refs_3_, bf16[48,4096]{1,0:T(8,128)(2,1)S(1)} %get-tuple-element.17.refs_2_.refs_1_), custom_call_target="tpu_custom_call" | custom-call | flops 939524096 | bytes 2097152 | tf_op jit(solution)/shard_map/pallas_call | solution.py:122
  6.2 0.0 collective-permute-done.refs_1_
  6.2 0.0 copy-done
  6.2 4.4 %shard_map.39 = bf16[4,64,512]{2,1,0:T(8,128)(2,1)} custom-call(s32[1]{0:T(128)} %bitcast.refs_0_, bf16[112,2048]{1,0:T(8,128)(2,1)S(1)} %collective-permute-done.refs_1_, bf16[48,4096]{1,0:T(8,128)(2,1)S(1)} %get-tuple-element.17.refs_2_.refs_1_, f32[64,2048]{1,0:T(8,128)S(1)} %shard_map.38.refs_3_), custom_call_target="tpu_custom_call" | custom-call | flops 939524096 | bytes 2097152 | tf_op jit(solution)/shard_map/pallas_call | solution.py:122
  10.6 6.7 %all-to-all-start = ((bf16[4,64,512]{2,1,0:T(8,128)(2,1)}), bf16[4,64,512]{2,1,0:T(8,128)(2,1)S(1)}, u32[]{:S(2)}, u32[]{:S(2)}) async-start(bf16[4,64,512]{2,1,0:T(8,128)(2,1)} %shard_map.39), calls=%async_computation | async-start | bytes 524288 | tf_op jit(solution)/shard_map/all_to_all | solution.py:179
  17.3 0.0 collective-permute-done.1.refs_0_
  17.3 0.0 collective-permute-start.2
  17.3 3.7 %shard_map.40.refs_2_ = f32[64,2048]{1,0:T(8,128)S(1)} custom-call(bf16[112,2048]{1,0:T(8,128)(2,1)S(1)} %collective-permute-done.1.refs_0_, bf16[112,2048]{1,0:T(8,128)(2,1)S(1)} %get-tuple-element.18.refs_1_.refs_3_), custom_call_target="tpu_custom_call" | custom-call | flops 939524096 | bytes 2097152 | tf_op jit(solution)/shard_map/pallas_call | solution.py:122
  21.0 5.6 %all-to-all-done = bf16[4,64,512]{2,1,0:T(8,128)(2,1)S(1)} async-done(((bf16[4,64,512]{2,1,0:T(8,128)(2,1)}), bf16[4,64,512]{2,1,0:T(8,128)(2,1)S(1)}, u32[]{:S(2)}, u32[]{:S(2)}) %all-to-all-start) | async-done | bytes 262176 | tf_op jit(solution)/shard_map/all_to_all | solution.py:179
  26.6 0.7 broadcast_in_dim.4
  27.3 3.6 %all-to-all-start.1 = ((bf16[4,64,512]{2,1,0:T(8,128)(2,1)}), bf16[4,64,512]{2,1,0:T(8,128)(2,1)S(1)}, u32[]{:S(2)}, u32[]{:S(2)}) async-start(bf16[4,64,512]{2,1,0:T(8,128)(2,1)} %broadcast_in_dim.4), calls=%async_computation.1 | async-start | bytes 524288 | tf_op jit(solution)/shard_map/all_to_all | solution.py:185
  30.9 0.0 copy-start.1
  30.9 0.0 collective-permute-done.2.refs_0_
  30.9 3.7 %shard_map.41.refs_4_ = f32[64,2048]{1,0:T(8,128)S(1)} custom-call(bf16[112,2048]{1,0:T(8,128)(2,1)S(1)} %collective-permute-done.2.refs_0_, bf16[112,2048]{1,0:T(8,128)(2,1)S(1)} %get-tuple-element.18.refs_1_.refs_3_, f32[64,2048]{1,0:T(8,128)S(1)} %shard_map.40.refs_2_), custom_call_target="tpu_custom_call" | custom-call | flops 939524096 | bytes 2097152 | tf_op jit(solution)/shard_map/pallas_call | solution.py:122
  34.6 4.8 %all-to-all-done.1.refs_2_ = bf16[4,64,512]{2,1,0:T(8,128)(2,1)S(1)} async-done(((bf16[4,64,512]{2,1,0:T(8,128)(2,1)}), bf16[4,64,512]{2,1,0:T(8,128)(2,1)S(1)}, u32[]{:S(2)}, u32[]{:S(2)}) %all-to-all-start.1) | async-done | bytes 262176 | tf_op jit(solution)/shard_map/all_to_all | solution.py:185
  39.5 0.0 collective-permute-start.3
  39.5 0.0 copy-done.1
  39.5 3.7 %shard_map.42.refs_4_ = f32[64,2048]{1,0:T(8,128)S(1)} custom-call(s32[1]{0:T(128)} %bitcast.refs_0_, bf16[48,4096]{1,0:T(8,128)(2,1)S(1)} %copy-done.1, bf16[4,64,512]{2,1,0:T(8,128)(2,1)S(1)} %all-to-all-done.1.refs_2_, bf16[112,2048]{1,0:T(8,128)(2,1)S(1)} %get-tuple-element.18.refs_1_.refs_3_, f32[64,2048]{1,0:T(8,128)S(1)} %shard_map.41.refs_4_), custom_call_target="tpu_custom_call" | custom-call | flops 939524096 | bytes 2097152 | tf_op jit(solution)/shard_map/pallas_call | solution.py:122
  43.1 0.0 collective-permute-done.3.refs_2_
  43.1 3.7 %shard_map.43 = f32[4,64,512]{2,1,0:T(8,128)S(1)} custom-call(s32[1]{0:T(128)S(6)} %sub.3.refs_0_, bf16[48,4096]{1,0:T(8,128)(2,1)S(1)} %copy-done.1, bf16[4,64,512]{2,1,0:T(8,128)(2,1)S(1)} %collective-permute-done.3.refs_2_, bf16[112,2048]{1,0:T(8,128)(2,1)S(1)} %get-tuple-element.18.refs_1_.refs_3_, f32[64,2048]{1,0:T(8,128)S(1)} %shard_map.42.refs_4_), custom_call_target="tpu_custom_call" | custom-call | flops 939524096 | bytes 2097152 | tf_op jit(solution)/shard_map/pallas_call | solution.py:122
  46.8 13.8 %all_to_all.20 = f32[4,64,512]{2,1,0:T(8,128)S(1)} all-to-all(f32[4,64,512]{2,1,0:T(8,128)S(1)} %shard_map.43), channel_id=1, replica_groups=mesh['dp'=4,'centers'=8] {'dp'}, dimensions={0} | all-to-all | bytes 1048576 | tf_op jit(solution)/shard_map/all_to_all | solution.py:196
  60.6 0.1 broadcast_in_dim.5
  60.6 10.4 %all_to_all.21 = f32[4,64,512]{2,1,0:T(8,128)S(1)} all-to-all(f32[4,64,512]{2,1,0:T(8,128)S(1)} %broadcast_in_dim.5), channel_id=1, replica_groups=mesh['dp'=4,'centers'=8] {'dp'}, dimensions={0} | all-to-all | bytes 1048576 | tf_op jit(solution)/shard_map/all_to_all | solution.py:198
  71.0 0.8 %copy.5 = f32[4,8,8,512]{3,2,0,1:T(8,128)} copy(f32[4,8,8,512]{3,2,1,0:T(8,128)S(1)} %bitcast.7) | data formatting | bytes 1048576 | tf_op jit(solution)/shard_map/reshape | solution.py:199
  (2 shorter events, 0.1 us)
Async XLA Ops:
  1.3 5.0 %copy-start = (bf16[48,4096]{1,0:T(8,128)(2,1)}, bf16[48,4096]{1,0:T(8,128)(2,1)S(1)}, u32[]{:S(2)}) copy-start(bf16[48,4096]{1,0:T(8,128)(2,1)S(1)} %get-tuple-element.17.refs_2_.refs_1_) | copy-start | bytes 1179652
  1.3 4.9 %collective-permute-start = (bf16[112,2048]{1,0:T(8,128)(2,1)S(1)}, bf16[112,2048]{1,0:T(8,128)(2,1)S(1)}, u32[]{:S(2)}, u32[]{:S(2)}) collective-permute-start(bf16[112,2048]{1,0:T(8,128)(2,1)S(1)} %get-tuple-element.18.refs_1_.refs_3_), channel_id=1, source_target_pairs={{0,1},{1,0},{2,3},{3,2},{4,5},{5,4},{6,7},{7,6},{8,9},{9,8},{10,11... | collective-permute-start | bytes 1376264 | tf_op jit(solution)/shard_map/ppermute | solution.py:163
  1.8 15.4 %collective-permute-start.1 = (bf16[112,2048]{1,0:T(8,128)(2,1)S(1)}, bf16[112,2048]{1,0:T(8,128)(2,1)S(1)}, u32[]{:S(2)}, u32[]{:S(2)}) collective-permute-start(bf16[112,2048]{1,0:T(8,128)(2,1)S(1)} %get-tuple-element.18.refs_1_.refs_3_), channel_id=1, source_target_pairs={{0,0},{1,1},{4,2},{5,3},{2,4},{3,5},{6,6},{7,7},{10,8},{11,9},{14,... | collective-permute-start | bytes 1376264 | tf_op jit(solution)/shard_map/ppermute | solution.py:164
  10.6 15.9 %all-to-all-start = ((bf16[4,64,512]{2,1,0:T(8,128)(2,1)}), bf16[4,64,512]{2,1,0:T(8,128)(2,1)S(1)}, u32[]{:S(2)}, u32[]{:S(2)}) async-start(bf16[4,64,512]{2,1,0:T(8,128)(2,1)} %shard_map.39), calls=%async_computation | async-start | bytes 524288 | tf_op jit(solution)/shard_map/all_to_all | solution.py:179
  17.3 13.6 %collective-permute-start.2 = (bf16[112,2048]{1,0:T(8,128)(2,1)S(1)}, bf16[112,2048]{1,0:T(8,128)(2,1)S(1)}, u32[]{:S(2)}, u32[]{:S(2)}) collective-permute-start(bf16[112,2048]{1,0:T(8,128)(2,1)S(1)} %collective-permute-done.1.refs_0_), channel_id=1, source_target_pairs={{1,0},{0,1},{3,2},{2,3},{5,4},{4,5},{7,6},{6,7},{9,8},{8,9},{11,10... | collective-permute-start | bytes 1376264 | tf_op jit(solution)/shard_map/ppermute | solution.py:177
  27.3 12.1 %all-to-all-start.1 = ((bf16[4,64,512]{2,1,0:T(8,128)(2,1)}), bf16[4,64,512]{2,1,0:T(8,128)(2,1)S(1)}, u32[]{:S(2)}, u32[]{:S(2)}) async-start(bf16[4,64,512]{2,1,0:T(8,128)(2,1)} %broadcast_in_dim.4), calls=%async_computation.1 | async-start | bytes 524288 | tf_op jit(solution)/shard_map/all_to_all | solution.py:185
  30.9 8.5 %copy-start.1 = (bf16[48,4096]{1,0:T(8,128)(2,1)S(1)}, bf16[48,4096]{1,0:T(8,128)(2,1)}, u32[]{:S(2)}) copy-start(bf16[48,4096]{1,0:T(8,128)(2,1)} %copy-done) | copy-start | bytes 1179652
  39.5 3.7 %collective-permute-start.3 = (bf16[4,64,512]{2,1,0:T(8,128)(2,1)S(1)}, bf16[4,64,512]{2,1,0:T(8,128)(2,1)S(1)}, u32[]{:S(2)}, u32[]{:S(2)}) collective-permute-start(bf16[4,64,512]{2,1,0:T(8,128)(2,1)S(1)} %all-to-all-done.1.refs_2_), channel_id=1, source_target_pairs={{0,1},{1,0},{2,3},{3,2},{4,5},{5,4},{6,7},{7,6},{8,9},{9,8},{10,11... | collective-permute-start | bytes 786440 | tf_op jit(solution)/shard_map/ppermute | solution.py:189
